TPU v7x, 128 devices: a whole 4x4x4 slice. The times are simulated.
128 devices in a mesh: member: 16 (over z, x_lo, core), space: 8 (over x_hi, y).
Axes of the slice: x: 4 (x_hi: 2, x_lo: 2; x = x_hi * 2 + x_lo), y: 4, z: 4, core: 2. Of those that a mesh axis runs over, the one named last changes fastest.
Arguments:
- weather: bfloat16 [16, 84, 256, 1440], P('member', None, 'space'), may hold values from -6 to 6
- coefficients: int32 [16, 84, 2, 368, 361], P('member', None, None, 'space'), may hold values from -1073741824 to 1073741823
- channel_scale: float32 [84], replicated, may hold values from 0.3 to 3
Outputs:
- perturbed: bfloat16 [16, 84, 256, 1440], P('member', None, 'space')
All inputs are finite; a program needn't handle non-finite values.
Results may differ from a plain program's by a relative error of at most 0.007.
Values may be sent and summed in bfloat16 or wider, within the bound.
No kernel may reach another device: no remote copies, remote signals or barrier semaphores. Data moves between devices by JAX's collectives and lax.ppermute only.
A program may use at most 192 MiB of HBM per device.

v0:
```python
import functools
import math

import jax
import jax.numpy as jnp
from jax import lax
from jax.experimental import pallas as pl
from jax.experimental.pallas import tpu as pltpu
from jax.sharding import PartitionSpec as P


F32 = jnp.float32
BF16 = jnp.bfloat16
SLOTS = 48
LEG_PITCH = 369
UNI_PITCH = 49
LEG_UNROLL = 16
EARLY = 10
VMEM = 60 * 2**20


def relative_part(part, me):
    return ((part ^ me) & 1) * 8 + ((part // 4 - me // 4) & 3) * 2 + (((part ^ me) // 2) & 1)


def synthesis_kernel(first_ref, table_ref, coef_hbm, first_hbm, rest_hbm, away_hbm, coef, leg, uni, out_ref, sems):
    channels, order_local, _, degree_count = coef.shape
    pairs = 2 * channels
    fetch = pltpu.make_async_copy(coef_hbm, coef, sems.at[0])
    fetch.start()
    me = first_ref[1]
    order = lax.broadcasted_iota(jnp.int32, (SLOTS, 128), 0) + first_ref[0]
    order_square = order.astype(F32) * order.astype(F32)
    cosine = [jnp.broadcast_to(table_ref[0:1, 128 * h : 128 * h + 128], (SLOTS, 128)) for h in range(2)]
    diagonal = [table_ref[8 : 8 + SLOTS, 128 * h : 128 * h + 128] for h in range(2)]
    uni[0, 0:SLOTS, :] = jnp.zeros((SLOTS, 128), F32)
    empty = uni[0, 0:SLOTS, :]

    def advance(degree, carry):
        older, newer, down = carry
        value = jnp.full((8, 128), degree, jnp.int32).astype(F32)
        square = value * value
        inverse = 1.0 / (4.0 * square - 1.0)
        square = jnp.concatenate([square] * (SLOTS // 8))
        inverse = jnp.concatenate([inverse] * (SLOTS // 8))
        ratio = jnp.maximum((square - order_square) * inverse, 1e-30)
        up = lax.rsqrt(ratio)
        hit = order == degree
        made = []
        for h in range(2):
            row = jnp.where(hit, diagonal[h], up * (cosine[h] * newer[h] - down * older[h]))
            leg[h, pl.ds(degree, SLOTS, stride=LEG_PITCH), :] = row
            made.append(row)
        return newer, tuple(made), ratio * up

    def advance_some(turn, carry):
        for u in range(LEG_UNROLL):
            carry = advance(turn * LEG_UNROLL + u, carry)
        return carry

    lax.fori_loop(0, -(-degree_count // LEG_UNROLL), advance_some, ((empty, empty), (empty, empty), empty))
    fetch.wait()
    factor = math.sqrt(3.0) * math.sqrt(4.0 * math.pi) / degree_count * 2.0 ** (-30)

    def sum_degrees(m):
        spectral = (coef[:, m, :, :].astype(F32) * factor).reshape(pairs, degree_count).astype(BF16)
        halves = [leg[h, pl.ds(m * LEG_PITCH, degree_count), :].astype(BF16) for h in range(2)]
        fourier = jnp.dot(spectral, jnp.concatenate(halves, axis=1), preferred_element_type=F32)
        for h in range(2):
            uni[h, pl.ds(m, pairs, stride=UNI_PITCH), :] = fourier[:, 128 * h : 128 * h + 128]

    def sum_two(turn, carry):
        sum_degrees(2 * turn)
        sum_degrees(2 * turn + 1)
        return carry

    lax.fori_loop(0, order_local // 2, sum_two, 0)
    blank = jnp.zeros((pairs, 128), F32)
    for h in range(2):
        for m in range(order_local, SLOTS):
            uni[h, pl.ds(m, pairs, stride=UNI_PITCH), :] = blank
    lane_group = lax.broadcasted_iota(jnp.int32, (2 * SLOTS, 128), 1) // 32

    def regroup(q, carry):
        for h in range(2):
            parts = [
                jnp.concatenate([uni[h, pl.ds((8 * q + 2 * i + p) * UNI_PITCH, SLOTS), :] for p in range(2)])
                for i in range(4)
            ]
            for group in range(4):
                joined = None
                for i in range(4):
                    turn = (i - group) % 4
                    moved = parts[i] if turn == 0 else pltpu.roll(parts[i], 32 * turn, 1)
                    joined = moved if joined is None else jnp.where(lane_group == i, moved, joined)
                joined = joined.astype(BF16)
                for j in range(3):
                    t = 3 * q + j
                    row = pl.multiple_of(32 * (t % 4), 32)
                    out_ref[4 * h + group, relative_part(t // 4, me), pl.ds(row, 32), :] = joined[32 * j : 32 * j + 32]
        return carry

    def store(part, act):
        place = relative_part(part, me)

        @pl.when(place < EARLY)
        def _():
            act(pltpu.make_async_copy(out_ref.at[:, place], first_hbm.at[:, place], sems.at[1 + part]))

        @pl.when(place >= EARLY)
        def _():
            act(pltpu.make_async_copy(out_ref.at[:, place], rest_hbm.at[:, place - EARLY], sems.at[1 + part]))

        @pl.when(place >= 8)
        def _():
            act(pltpu.make_async_copy(out_ref.at[:, place], away_hbm.at[:, place - 8], sems.at[17 + part]))

    done = 0
    for first, last in ((0, 6), (6, 12), (12, 18), (18, channels // 4)):
        lax.fori_loop(first, last, regroup, 0, unroll=3)
        if last == channels // 4:
            for s in range(8):
                out_ref[s, relative_part(15, me), 96:128, :] = jnp.zeros((32, 128), BF16)
        whole = 16 if last == channels // 4 else 3 * last // 4
        for part in range(done, whole):
            store(part, lambda copy: copy.start())
        done = whole
    for part in range(16):
        store(part, lambda copy: copy.wait())


def summed(parts):
    return functools.reduce(lambda a, b: a + b, [part.astype(F32) for part in parts])


def perturb_kernel(groups, scale_ref, me_ref, basis_ref, weather_ref, *refs):
    row_refs, mean_refs, out_ref, centred = refs[:2], refs[2:12], refs[12], refs[13]
    step = pl.program_id(0)
    me = me_ref[1]

    @pl.when(step == 0)
    def _():
        places = ((0, 0), (0, 1), (1, 0), (1, 1), (2, 0), (3, 0), (4, 0), (4, 1))
        for i in range(16):
            piece, dx = places[i % 8]
            for s in range(8):
                row = row_refs[0][s, i] if i < EARLY else row_refs[1][s, i - EARLY]
                value = row.astype(F32) - mean_refs[5 * (i // 8) + piece][s, dx].astype(F32)
                centred[s, i] = value.astype(BF16)

    columns = []
    for g in range(groups):
        pieces = []
        for s in range(8):
            for j in range(3):
                t = 3 * (step * groups + g) + j
                part = relative_part(t // 4, me)
                pieces.append(centred[s, part, pl.ds(pl.multiple_of(32 * (t % 4), 32), 32), :])
        columns.append(jnp.concatenate(pieces, axis=0))
    noise = lax.dot_general(
        jnp.concatenate(columns, axis=1), basis_ref[...], (((0,), (0,)), ((), ())), preferred_element_type=F32
    )
    for c in range(4 * groups):
        scale = scale_ref[step * 4 * groups + c]
        out_ref[c] = (weather_ref[c].astype(F32) + scale * noise[32 * c : 32 * c + 32]).astype(BF16)


def legendre_start(first_order, colatitude):
    orders = first_order + jnp.arange(SLOTS, dtype=jnp.int32)
    steps = jnp.arange(1, 384, dtype=jnp.int32)
    terms = 0.5 * jnp.log((2.0 * steps.astype(F32) + 1.0) / (2.0 * steps.astype(F32)))
    logs = jnp.sum(jnp.where(steps[None, :] <= orders[:, None], terms[None, :], 0.0), axis=1)
    diagonal = jnp.exp(
        logs[:, None]
        - 0.5 * math.log(4.0 * math.pi)
        + orders.astype(F32)[:, None] * jnp.log(jnp.sin(colatitude))[None, :]
    )
    cosine = jnp.broadcast_to(jnp.cos(colatitude)[None, :], (8, colatitude.shape[0]))
    return jnp.concatenate([cosine, diagonal])


def fourier_basis(bands, order_local, lon_count):
    slots = jnp.arange(SLOTS, dtype=jnp.int32)
    orders = order_local * jnp.arange(bands, dtype=jnp.int32)[:, None] + slots[None, :]
    columns = jnp.arange(lon_count, dtype=jnp.int32)
    phases = orders[:, :, None] * columns % lon_count
    angles = 2.0 * math.pi / lon_count * phases.astype(F32)
    weights = jnp.where(orders == 0, 1.0, math.sqrt(2.0))
    weights = jnp.where(slots[None, :] < order_local, weights, 0.0).astype(F32)[:, :, None]
    both = jnp.stack([weights * jnp.cos(angles), weights * jnp.sin(angles)], axis=1)
    return both.astype(BF16).reshape(bands * 2 * SLOTS, lon_count)


def local(weather, coefficients, channel_scale):
    members = lax.axis_size("member")
    bands = lax.axis_size("space")
    _, channels, rows_local, lon_count = weather.shape
    order_local, degree_count = coefficients.shape[3:]
    lat_count = rows_local * bands
    first_order = lax.axis_index("space") * order_local
    row_first = (lon_count // 2 + 1 - lat_count) // 2
    colatitude = math.pi * (row_first + jnp.arange(lat_count, dtype=jnp.int32)).astype(F32) / (lon_count // 2)
    vmem = pl.BlockSpec(memory_space=pltpu.VMEM)
    smem = pl.BlockSpec(memory_space=pltpu.SMEM)
    params = pltpu.CompilerParams(vmem_limit_bytes=VMEM)
    me = lax.axis_index("member")
    place = jnp.stack([first_order, me])
    ring = range(members)

    def to_core(x):
        return lax.ppermute(x, "member", [(e, e ^ 1) for e in ring])

    def to_chip(x):
        return lax.ppermute(x, "member", [(e, e ^ 2) for e in ring])

    def along_z(x, steps):
        return lax.ppermute(x, "member", [(e, (e + 4 * steps) % members) for e in ring])

    coef = jnp.transpose(coefficients[0], (0, 2, 1, 3))
    first, rest, away = pl.pallas_call(
        synthesis_kernel,
        in_specs=[smem, vmem, pl.BlockSpec(memory_space=pl.ANY)],
        out_specs=[pl.BlockSpec(memory_space=pl.ANY)] * 3,
        out_shape=[jax.ShapeDtypeStruct((bands, n, 128, 128), BF16) for n in (EARLY, members - EARLY, 8)],
        scratch_shapes=[
            pltpu.VMEM((channels, order_local, 2, degree_count), jnp.int32),
            pltpu.VMEM((2, SLOTS * LEG_PITCH + 8, 128), F32),
            pltpu.VMEM((2, 2 * channels * UNI_PITCH, 128), F32),
            pltpu.VMEM((bands, members, 128, 128), BF16),
            pltpu.SemaphoreType.DMA((33,)),
        ],
        compiler_params=params,
        name="synthesis",
    )(place, legendre_start(first_order, colatitude), coef)

    first_rows = lax.all_to_all(first, "space", split_axis=0, concat_axis=0, tiled=True)
    got = to_core(away)
    sums = [summed([x[:, 2 * d : 2 * d + 2] for x in (first, got)]).astype(BF16) for d in range(4)]
    far = sums[2]
    up = along_z(far[:, :1], 1)
    down = along_z(far[:, 1:], 3)
    up = jnp.concatenate([summed([sums[1][:, :1], up]).astype(BF16), sums[1][:, 1:]], axis=1)
    down = jnp.concatenate([sums[3][:, :1], summed([sums[3][:, 1:], down]).astype(BF16)], axis=1)
    arrived = [along_z(up, 1), along_z(down, 3)]
    basis, own = lax.optimization_barrier((fourier_basis(bands, order_local, lon_count), sums[0]))
    column = summed([own, *arrived]).astype(BF16)
    given = to_chip(column)[:, ::-1]
    mean = (summed([column, given]) * (1.0 / members)).astype(BF16)
    mean, first_rows = lax.optimization_barrier((mean, first_rows))
    mean = lax.all_to_all(mean, "space", split_axis=0, concat_axis=0, tiled=True)
    mean, rest = lax.optimization_barrier((mean, rest))
    last_rows = lax.all_to_all(rest, "space", split_axis=0, concat_axis=0, tiled=True)
    below = along_z(mean, 1)
    above = along_z(mean, 3)
    far_up = along_z(below[:, :1], 1)
    far_down = along_z(above[:, 1:], 3)
    other = [to_core(mean)]
    other.append(to_core(above))
    other += [to_core(far_up), to_core(far_down)]
    other.append(to_core(below))
    means = [mean, above, far_up, far_down, below, *other]

    groups = 7
    once = pl.Buffered(1)
    band = pl.BlockSpec((4 * groups, rows_local, lon_count), lambda i: (i, 0, 0))
    perturbed = pl.pallas_call(
        functools.partial(perturb_kernel, groups),
        grid=(channels // (4 * groups),),
        in_specs=[
            smem,
            smem,
            pl.BlockSpec(basis.shape, lambda i: (0, 0), pipeline_mode=once),
            band,
        ]
        + [pl.BlockSpec(x.shape, lambda i: (0, 0, 0, 0), pipeline_mode=once) for x in (first, rest, *means)],
        out_specs=band,
        out_shape=jax.ShapeDtypeStruct(weather.shape[1:], BF16),
        scratch_shapes=[pltpu.VMEM((bands, members, 128, 128), BF16)],
        compiler_params=pltpu.CompilerParams(vmem_limit_bytes=60 * 2**20),
        name="perturb",
    )(channel_scale, place, basis, weather[0], first_rows, last_rows, *means)
    return perturbed[None]


def solution(mesh):
    return jax.shard_map(
        local,
        mesh=mesh,
        in_specs=(P("member", None, "space", None), P("member", None, None, "space", None), P()),
        out_specs=P("member", None, "space", None),
        check_vma=False,
    )
```

profile of v0, /device:TPU:1, one launch (start us, length us, event | category | flops | bytes accessed | tf_op | source)
XLA Modules:
  0.0 134.2 jit_solution(11081372900761089704)
XLA Ops:
  0.1 0.2 select_reduce_fusion
  0.3 0.7 pad_add_fusion.first_ref.me_ref
  1.0 0.1 add_exponential_fusion
  1.1 0.6 pad_maximum_fusion.3.table_ref
  1.7 18.5 %synthesis.1 = (bf16[8,10,128,128]{3,2,1,0:T(8,128)(2,1)}, bf16[8,6,128,128]{3,2,1,0:T(8,128)(2,1)}, bf16[8,8,128,128]{3,2,1,0:T(8,128)(2,1)}) custom-call(s32[2]{0:T(128)} %pad_add_fusion.first_ref.me_ref, f32[56,256]{1,0:T(8,128)} %pad_maximum_fusion.3.table_ref, s32[84,46,2,361]{3,2,1,0:T(2,128)} %bitcast.8), custom_call_target="tpu_custom_call" | custom-call | tf_op jit(solution)/shard_map/synthesis/pallas_call | solution.py:220
  20.3 1.6 %collective-permute-start = (bf16[8,8,128,128]{3,2,1,0:T(8,128)(2,1)}, bf16[8,8,128,128]{3,2,1,0:T(8,128)(2,1)}, u32[]{:S(2)}, u32[]{:S(2)}) collective-permute-start(bf16[8,8,128,128]{3,2,1,0:T(8,128)(2,1)} %get-tuple-element.15), channel_id=1, source_target_pairs={{0,8},{8,0},{16,24},{24,16},{32,40},{40,32},{48,56},{56,48},{64,72... | collective-permute-start | bytes 6291464 | tf_op jit(solution)/shard_map/ppermute | solution.py:211
  21.8 6.8 %all-to-all-start = ((bf16[8,10,128,128]{3,2,1,0:T(8,128)(2,1)}), bf16[8,10,128,128]{3,2,1,0:T(8,128)(2,1)S(1)}, u32[]{:S(2)}, u32[]{:S(2)}) async-start(bf16[8,10,128,128]{3,2,1,0:T(8,128)(2,1)} %get-tuple-element.14), calls=%async_computation | async-start | bytes 5242880 | tf_op jit(solution)/shard_map/all_to_all | solution.py:236
  28.6 0.1 iota_add_fusion
  28.7 2.9 %add_convert_fusion.3 = (bf16[8,2,128,128]{3,2,1,0:T(8,128)(2,1)S(1)}, bf16[8,2,128,128]{3,2,1,0:T(8,128)(2,1)S(1)}, bf16[8,2,128,128]{3,2,1,0:T(8,128)(2,1)S(1)}, bf16[8,2,128,128]{3,2,1,0:T(8,128)(2,1)S(1)}) fusion(bf16[8,8,128,128]{3,2,1,0:T(8,128)(2,1)} %collective-permute-done, bf16[8,10,128,128]{3,2,1,0:T(8,128)(2,1)} %get-tuple-element.14), kind=kLoop, calls=%fused_computation.14 | loop fusion | flops 4194304 | bytes 6291456 | tf_op jit(solution)/shard_map/convert_element_type | solution.py:238
  31.7 3.8 %collective-permute-start.3 = (bf16[8,1,128,128]{3,2,1,0:T(8,128)(2,1)S(1)}, bf16[8,1,128,128]{3,2,1,0:T(8,128)(2,1)S(1)}, u32[]{:S(2)}, u32[]{:S(2)}) collective-permute-start(bf16[8,1,128,128]{3,2,1,0:T(8,128)(2,1)S(1)} %get-tuple-element.28), channel_id=1, source_target_pairs={{0,96},{8,104},{16,112},{24,120},{32,0},{40,8},{48,16},{56,24},{64... | collective-permute-start | bytes 786440 | tf_op jit(solution)/shard_map/ppermute | solution.py:217
  35.4 0.1 select_select_fusion
  35.6 0.1 collective-permute-start.1
  35.7 5.1 %collective-permute-done.3 = bf16[8,1,128,128]{3,2,1,0:T(8,128)(2,1)S(1)} collective-permute-done((bf16[8,1,128,128]{3,2,1,0:T(8,128)(2,1)S(1)}, bf16[8,1,128,128]{3,2,1,0:T(8,128)(2,1)S(1)}, u32[]{:S(2)}, u32[]{:S(2)}) %collective-permute-start.3) | collective-permute-done | bytes 262176 | tf_op jit(solution)/shard_map/ppermute | solution.py:217
  40.8 0.1 add_convert_fusion.5
  40.9 0.1 pad_maximum_fusion.2
  40.9 3.5 %collective-permute-start.4 = (bf16[8,2,128,128]{3,2,1,0:T(8,128)(2,1)S(1)}, bf16[8,2,128,128]{3,2,1,0:T(8,128)(2,1)S(1)}, u32[]{:S(2)}, u32[]{:S(2)}) collective-permute-start(bf16[8,2,128,128]{3,2,1,0:T(8,128)(2,1)S(1)} %pad_maximum_fusion.2), channel_id=1, source_target_pairs={{0,96},{8,104},{16,112},{24,120},{32,0},{40,8},{48,16},{56,24},{64... | collective-permute-start | bytes 1572872 | tf_op jit(solution)/shard_map/ppermute | solution.py:217
  44.4 0.0 collective-permute-done.1
  44.4 0.1 add_convert_fusion.6
  44.5 0.1 pad_maximum_fusion.1
  44.6 0.1 collective-permute-start.2
  44.6 10.7 %multiply_convert_fusion.1 = (bf16[8,1,48,1440]{3,2,1,0:T(8,128)(2,1)S(1)}, bf16[8,1,48,1440]{3,2,1,0:T(8,128)(2,1)S(1)}) fusion(s32[8,48]{1,0:T(8,128)S(1)} %iota_add_fusion, f32[8,48]{1,0:T(8,128)S(1)} %select_select_fusion), kind=kLoop, calls=%fused_computation.5 | loop fusion | flops 7188480 | bytes 2214912 | tf_op jit(solution)/shard_map/convert
  55.4 1.7 %pad_maximum_fusion = bf16[8,2,48,1440]{3,2,1,0:T(8,128)(2,1)} fusion(bf16[8,1,48,1440]{3,2,1,0:T(8,128)(2,1)S(1)} %get-tuple-element.30, bf16[8,1,48,1440]{3,2,1,0:T(8,128)(2,1)S(1)} %get-tuple-element.29), kind=kLoop, calls=%fused_computation.3 | loop fusion | flops 1105920 | bytes 4423680 | tf_op jit(solution)/shard_map/stack | solution.py:190
  57.0 0.0 collective-permute-done.4
  57.0 0.9 collective-permute-done.2
  57.9 0.2 add_convert_fusion
  58.1 0.4 collective-permute-start.5
  58.5 10.8 %collective-permute-done.5 = bf16[8,2,128,128]{3,2,1,0:T(8,128)(2,1)S(1)} collective-permute-done((bf16[8,2,128,128]{3,2,1,0:T(8,128)(2,1)S(1)}, bf16[8,2,128,128]{3,2,1,0:T(8,128)(2,1)S(1)}, u32[]{:S(2)}, u32[]{:S(2)}) %collective-permute-start.5) | collective-permute-done | bytes 524320 | tf_op jit(solution)/shard_map/ppermute | solution.py:214
  69.4 1.0 multiply_convert_fusion.2
  70.3 0.0 all-to-all-done.refs_0_
  70.3 14.9 %all_to_all.15.refs_2_ = bf16[8,2,128,128]{3,2,1,0:T(8,128)(2,1)S(1)} all-to-all(bf16[8,2,128,128]{3,2,1,0:T(8,128)(2,1)} %multiply_convert_fusion.2), channel_id=1, replica_groups=mesh['member'=16,'space'=8] {'space'}, dimensions={0} | all-to-all | bytes 1048576 | tf_op jit(solution)/shard_map/all_to_all | solution.py:250
  85.3 4.3 %all-to-all-start.2 = ((bf16[8,6,128,128]{3,2,1,0:T(8,128)(2,1)}), bf16[8,6,128,128]{3,2,1,0:T(8,128)(2,1)}, u32[]{:S(2)}, u32[]{:S(2)}) async-start(bf16[8,6,128,128]{3,2,1,0:T(8,128)(2,1)} %get-tuple-element.21), calls=%async_computation.2 | async-start | bytes 3145728 | tf_op jit(solution)/shard_map/all_to_all | solution.py:252
  89.6 2.2 %collective-permute-start.7 = (bf16[8,2,128,128]{3,2,1,0:T(8,128)(2,1)S(1)}, bf16[8,2,128,128]{3,2,1,0:T(8,128)(2,1)S(1)}, u32[]{:S(2)}, u32[]{:S(2)}) collective-permute-start(bf16[8,2,128,128]{3,2,1,0:T(8,128)(2,1)S(1)} %all_to_all.15.refs_2_), channel_id=1, source_target_pairs={{0,32},{8,40},{16,48},{24,56},{32,64},{40,72},{48,80},{56,88},{64,... | collective-permute-start | bytes 1572872 | tf_op jit(solution)/shard_map/ppermute | solution.py:217
  91.8 1.7 %collective-permute-start.6 = (bf16[8,2,128,128]{3,2,1,0:T(8,128)(2,1)S(1)}, bf16[8,2,128,128]{3,2,1,0:T(8,128)(2,1)S(1)}, u32[]{:S(2)}, u32[]{:S(2)}) collective-permute-start(bf16[8,2,128,128]{3,2,1,0:T(8,128)(2,1)S(1)} %all_to_all.15.refs_2_), channel_id=1, source_target_pairs={{0,96},{8,104},{16,112},{24,120},{32,0},{40,8},{48,16},{56,24},{64... | collective-permute-start | bytes 1572872 | tf_op jit(solution)/shard_map/ppermute | solution.py:217
  93.6 4.1 %collective-permute-start.10 = (bf16[8,2,128,128]{3,2,1,0:T(8,128)(2,1)S(1)}, bf16[8,2,128,128]{3,2,1,0:T(8,128)(2,1)S(1)}, u32[]{:S(2)}, u32[]{:S(2)}) collective-permute-start(bf16[8,2,128,128]{3,2,1,0:T(8,128)(2,1)S(1)} %all_to_all.15.refs_2_), channel_id=1, source_target_pairs={{0,8},{8,0},{16,24},{24,16},{32,40},{40,32},{48,56},{56,48},{64,72... | collective-permute-start | bytes 1572872 | tf_op jit(solution)/shard_map/ppermute | solution.py:211
  97.6 4.4 %collective-permute-done.7.refs_6_ = bf16[8,2,128,128]{3,2,1,0:T(8,128)(2,1)S(1)} collective-permute-done((bf16[8,2,128,128]{3,2,1,0:T(8,128)(2,1)S(1)}, bf16[8,2,128,128]{3,2,1,0:T(8,128)(2,1)S(1)}, u32[]{:S(2)}, u32[]{:S(2)}) %collective-permute-start.7) | collective-permute-done | bytes 524320 | tf_op jit(solution)/shard_map/ppermute | solution.py:217
  102.1 0.8 collective-permute-start.8
  102.8 4.6 %collective-permute-start.14 = (bf16[8,2,128,128]{3,2,1,0:T(8,128)(2,1)S(1)}, bf16[8,2,128,128]{3,2,1,0:T(8,128)(2,1)S(1)}, u32[]{:S(2)}, u32[]{:S(2)}) collective-permute-start(bf16[8,2,128,128]{3,2,1,0:T(8,128)(2,1)S(1)} %collective-permute-done.7.refs_6_), channel_id=1, source_target_pairs={{0,8},{8,0},{16,24},{24,16},{32,40},{40,32},{48,56},{56,48},{64,72... | collective-permute-start | bytes 1572872 | tf_op jit(solution)/shard_map/ppermute | solution.py:211
  107.4 0.1 collective-permute-start.11
  107.5 2.1 %collective-permute-start.9 = (bf16[8,1,128,128]{3,2,1,0:T(8,128)(2,1)S(1)}, bf16[8,1,128,128]{3,2,1,0:T(8,128)(2,1)S(1)}, u32[]{:S(2)}, u32[]{:S(2)}) collective-permute-start(bf16[8,1,128,128]{3,2,1,0:T(8,128)(2,1)S(1)} %slice.75), channel_id=1, source_target_pairs={{0,96},{8,104},{16,112},{24,120},{32,0},{40,8},{48,16},{56,24},{64... | collective-permute-start | bytes 786440 | tf_op jit(solution)/shard_map/ppermute | solution.py:217
  109.6 4.4 %collective-permute-start.12 = (bf16[8,1,128,128]{3,2,1,0:T(8,128)(2,1)S(1)}, bf16[8,1,128,128]{3,2,1,0:T(8,128)(2,1)S(1)}, u32[]{:S(2)}, u32[]{:S(2)}) collective-permute-start(bf16[8,1,128,128]{3,2,1,0:T(8,128)(2,1)S(1)} %collective-permute-done.8.refs_4_), channel_id=1, source_target_pairs={{0,8},{8,0},{16,24},{24,16},{32,40},{40,32},{48,56},{56,48},{64,72... | collective-permute-start | bytes 786440 | tf_op jit(solution)/shard_map/ppermute | solution.py:211
  114.0 2.0 %collective-permute-done.9.refs_5_ = bf16[8,1,128,128]{3,2,1,0:T(8,128)(2,1)S(1)} collective-permute-done((bf16[8,1,128,128]{3,2,1,0:T(8,128)(2,1)S(1)}, bf16[8,1,128,128]{3,2,1,0:T(8,128)(2,1)S(1)}, u32[]{:S(2)}, u32[]{:S(2)}) %collective-permute-start.9) | collective-permute-done | bytes 262176 | tf_op jit(solution)/shard_map/ppermute | solution.py:217
  116.1 1.0 collective-permute-start.13
  117.1 0.8 copy-done.4
  117.9 0.3 collective-permute-done.13.refs_10_
  118.3 0.4 copy-done.6
  118.7 0.1 copy-done.9
  118.8 0.1 copy-done.10
  118.9 15.2 %perturb.1 = bf16[84,32,1440]{2,1,0:T(8,128)(2,1)} custom-call(f32[84]{0:T(128)} %scale_ref.1, s32[2]{0:T(128)} %pad_add_fusion.first_ref.me_ref, bf16[768,1440]{1,0:T(8,128)(2,1)} %bitcast.9, bf16[84,32,1440]{2,1,0:T(8,128)(2,1)} %bitcast.10, bf16[8,10,128,128]{3,2,1,0:T(8,128)(2,1)} %copy-done, bf16[8,6,128,128]{3,2,1,0:T(8,128)(2,1)} %all-to-all-done.2.refs_1_, ...), custom_call_target="tpu_custom_call" | custom-call | tf_op jit(solution)/shard_map/perturb/pallas_call | solution.py:266
  (40 shorter events, 0.3 us)
Async XLA Ops:
  20.3 8.4 %collective-permute-start = (bf16[8,8,128,128]{3,2,1,0:T(8,128)(2,1)}, bf16[8,8,128,128]{3,2,1,0:T(8,128)(2,1)}, u32[]{:S(2)}, u32[]{:S(2)}) collective-permute-start(bf16[8,8,128,128]{3,2,1,0:T(8,128)(2,1)} %get-tuple-element.15), channel_id=1, source_target_pairs={{0,8},{8,0},{16,24},{24,16},{32,40},{40,32},{48,56},{56,48},{64,72... | collective-permute-start | bytes 6291464 | tf_op jit(solution)/shard_map/ppermute | solution.py:211
  21.8 48.5 %all-to-all-start = ((bf16[8,10,128,128]{3,2,1,0:T(8,128)(2,1)}), bf16[8,10,128,128]{3,2,1,0:T(8,128)(2,1)S(1)}, u32[]{:S(2)}, u32[]{:S(2)}) async-start(bf16[8,10,128,128]{3,2,1,0:T(8,128)(2,1)} %get-tuple-element.14), calls=%async_computation | async-start | bytes 5242880 | tf_op jit(solution)/shard_map/all_to_all | solution.py:236
  31.7 9.1 %collective-permute-start.3 = (bf16[8,1,128,128]{3,2,1,0:T(8,128)(2,1)S(1)}, bf16[8,1,128,128]{3,2,1,0:T(8,128)(2,1)S(1)}, u32[]{:S(2)}, u32[]{:S(2)}) collective-permute-start(bf16[8,1,128,128]{3,2,1,0:T(8,128)(2,1)S(1)} %get-tuple-element.28), channel_id=1, source_target_pairs={{0,96},{8,104},{16,112},{24,120},{32,0},{40,8},{48,16},{56,24},{64... | collective-permute-start | bytes 786440 | tf_op jit(solution)/shard_map/ppermute | solution.py:217
  35.6 8.8 %collective-permute-start.1 = (bf16[8,1,128,128]{3,2,1,0:T(8,128)(2,1)S(1)}, bf16[8,1,128,128]{3,2,1,0:T(8,128)(2,1)S(1)}, u32[]{:S(2)}, u32[]{:S(2)}) collective-permute-start(bf16[8,1,128,128]{3,2,1,0:T(8,128)(2,1)S(1)} %get-tuple-element.27), channel_id=1, source_target_pairs={{0,32},{8,40},{16,48},{24,56},{32,64},{40,72},{48,80},{56,88},{64,... | collective-permute-start | bytes 786440 | tf_op jit(solution)/shard_map/ppermute | solution.py:217
  40.9 16.1 %collective-permute-start.4 = (bf16[8,2,128,128]{3,2,1,0:T(8,128)(2,1)S(1)}, bf16[8,2,128,128]{3,2,1,0:T(8,128)(2,1)S(1)}, u32[]{:S(2)}, u32[]{:S(2)}) collective-permute-start(bf16[8,2,128,128]{3,2,1,0:T(8,128)(2,1)S(1)} %pad_maximum_fusion.2), channel_id=1, source_target_pairs={{0,96},{8,104},{16,112},{24,120},{32,0},{40,8},{48,16},{56,24},{64... | collective-permute-start | bytes 1572872 | tf_op jit(solution)/shard_map/ppermute | solution.py:217
  44.6 13.3 %collective-permute-start.2 = (bf16[8,2,128,128]{3,2,1,0:T(8,128)(2,1)S(1)}, bf16[8,2,128,128]{3,2,1,0:T(8,128)(2,1)S(1)}, u32[]{:S(2)}, u32[]{:S(2)}) collective-permute-start(bf16[8,2,128,128]{3,2,1,0:T(8,128)(2,1)S(1)} %pad_maximum_fusion.1), channel_id=1, source_target_pairs={{0,32},{8,40},{16,48},{24,56},{32,64},{40,72},{48,80},{56,88},{64,... | collective-permute-start | bytes 1572872 | tf_op jit(solution)/shard_map/ppermute | solution.py:217
  58.1 11.3 %collective-permute-start.5 = (bf16[8,2,128,128]{3,2,1,0:T(8,128)(2,1)S(1)}, bf16[8,2,128,128]{3,2,1,0:T(8,128)(2,1)S(1)}, u32[]{:S(2)}, u32[]{:S(2)}) collective-permute-start(bf16[8,2,128,128]{3,2,1,0:T(8,128)(2,1)S(1)} %add_convert_fusion), channel_id=1, source_target_pairs={{0,16},{8,24},{16,0},{24,8},{32,48},{40,56},{48,32},{56,40},{64,80... | collective-permute-start | bytes 1572872 | tf_op jit(solution)/shard_map/ppermute | solution.py:214
  70.3 31.7 %copy-start = (bf16[8,10,128,128]{3,2,1,0:T(8,128)(2,1)}, bf16[8,10,128,128]{3,2,1,0:T(8,128)(2,1)S(1)}, u32[]{:S(2)}) copy-start(bf16[8,10,128,128]{3,2,1,0:T(8,128)(2,1)S(1)} %all-to-all-done.refs_0_) | copy-start | bytes 7864324
  85.3 33.0 %copy-start.1 = (bf16[8,2,128,128]{3,2,1,0:T(8,128)(2,1)}, bf16[8,2,128,128]{3,2,1,0:T(8,128)(2,1)S(1)}, u32[]{:S(2)}) copy-start(bf16[8,2,128,128]{3,2,1,0:T(8,128)(2,1)S(1)} %all_to_all.15.refs_2_) | copy-start | bytes 1572868
  85.3 33.0 %all-to-all-start.2 = ((bf16[8,6,128,128]{3,2,1,0:T(8,128)(2,1)}), bf16[8,6,128,128]{3,2,1,0:T(8,128)(2,1)}, u32[]{:S(2)}, u32[]{:S(2)}) async-start(bf16[8,6,128,128]{3,2,1,0:T(8,128)(2,1)} %get-tuple-element.21), calls=%async_computation.2 | async-start | bytes 3145728 | tf_op jit(solution)/shard_map/all_to_all | solution.py:252
  89.6 12.4 %collective-permute-start.7 = (bf16[8,2,128,128]{3,2,1,0:T(8,128)(2,1)S(1)}, bf16[8,2,128,128]{3,2,1,0:T(8,128)(2,1)S(1)}, u32[]{:S(2)}, u32[]{:S(2)}) collective-permute-start(bf16[8,2,128,128]{3,2,1,0:T(8,128)(2,1)S(1)} %all_to_all.15.refs_2_), channel_id=1, source_target_pairs={{0,32},{8,40},{16,48},{24,56},{32,64},{40,72},{48,80},{56,88},{64,... | collective-permute-start | bytes 1572872 | tf_op jit(solution)/shard_map/ppermute | solution.py:217
  91.8 15.6 %collective-permute-start.6 = (bf16[8,2,128,128]{3,2,1,0:T(8,128)(2,1)S(1)}, bf16[8,2,128,128]{3,2,1,0:T(8,128)(2,1)S(1)}, u32[]{:S(2)}, u32[]{:S(2)}) collective-permute-start(bf16[8,2,128,128]{3,2,1,0:T(8,128)(2,1)S(1)} %all_to_all.15.refs_2_), channel_id=1, source_target_pairs={{0,96},{8,104},{16,112},{24,120},{32,0},{40,8},{48,16},{56,24},{64... | collective-permute-start | bytes 1572872 | tf_op jit(solution)/shard_map/ppermute | solution.py:217
  93.6 23.5 %collective-permute-start.10 = (bf16[8,2,128,128]{3,2,1,0:T(8,128)(2,1)S(1)}, bf16[8,2,128,128]{3,2,1,0:T(8,128)(2,1)S(1)}, u32[]{:S(2)}, u32[]{:S(2)}) collective-permute-start(bf16[8,2,128,128]{3,2,1,0:T(8,128)(2,1)S(1)} %all_to_all.15.refs_2_), channel_id=1, source_target_pairs={{0,8},{8,0},{16,24},{24,16},{32,40},{40,32},{48,56},{56,48},{64,72... | collective-permute-start | bytes 1572872 | tf_op jit(solution)/shard_map/ppermute | solution.py:211
  102.0 15.0 %copy-start.2 = (bf16[8,2,128,128]{3,2,1,0:T(8,128)(2,1)}, bf16[8,2,128,128]{3,2,1,0:T(8,128)(2,1)S(1)}, u32[]{:S(2)}) copy-start(bf16[8,2,128,128]{3,2,1,0:T(8,128)(2,1)S(1)} %collective-permute-done.7.refs_6_) | copy-start | bytes 1572868
  102.1 7.5 %collective-permute-start.8 = (bf16[8,1,128,128]{3,2,1,0:T(8,128)(2,1)S(1)}, bf16[8,1,128,128]{3,2,1,0:T(8,128)(2,1)S(1)}, u32[]{:S(2)}, u32[]{:S(2)}) collective-permute-start(bf16[8,1,128,128]{3,2,1,0:T(8,128)(2,1)S(1)} %slice.74), channel_id=1, source_target_pairs={{0,32},{8,40},{16,48},{24,56},{32,64},{40,72},{48,80},{56,88},{64,... | collective-permute-start | bytes 786440 | tf_op jit(solution)/shard_map/ppermute | solution.py:217
  102.8 14.2 %collective-permute-start.14 = (bf16[8,2,128,128]{3,2,1,0:T(8,128)(2,1)S(1)}, bf16[8,2,128,128]{3,2,1,0:T(8,128)(2,1)S(1)}, u32[]{:S(2)}, u32[]{:S(2)}) collective-permute-start(bf16[8,2,128,128]{3,2,1,0:T(8,128)(2,1)S(1)} %collective-permute-done.7.refs_6_), channel_id=1, source_target_pairs={{0,8},{8,0},{16,24},{24,16},{32,40},{40,32},{48,56},{56,48},{64,72... | collective-permute-start | bytes 1572872 | tf_op jit(solution)/shard_map/ppermute | solution.py:211
  107.4 9.7 %copy-start.3 = (bf16[8,2,128,128]{3,2,1,0:T(8,128)(2,1)}, bf16[8,2,128,128]{3,2,1,0:T(8,128)(2,1)S(1)}, u32[]{:S(2)}) copy-start(bf16[8,2,128,128]{3,2,1,0:T(8,128)(2,1)S(1)} %collective-permute-done.6.refs_3_) | copy-start | bytes 1572868
  107.4 9.7 %collective-permute-start.11 = (bf16[8,2,128,128]{3,2,1,0:T(8,128)(2,1)S(1)}, bf16[8,2,128,128]{3,2,1,0:T(8,128)(2,1)S(1)}, u32[]{:S(2)}, u32[]{:S(2)}) collective-permute-start(bf16[8,2,128,128]{3,2,1,0:T(8,128)(2,1)S(1)} %collective-permute-done.6.refs_3_), channel_id=1, source_target_pairs={{0,8},{8,0},{16,24},{24,16},{32,40},{40,32},{48,56},{56,48},{64,72... | collective-permute-start | bytes 1572872 | tf_op jit(solution)/shard_map/ppermute | solution.py:211
  107.5 8.5 %collective-permute-start.9 = (bf16[8,1,128,128]{3,2,1,0:T(8,128)(2,1)S(1)}, bf16[8,1,128,128]{3,2,1,0:T(8,128)(2,1)S(1)}, u32[]{:S(2)}, u32[]{:S(2)}) collective-permute-start(bf16[8,1,128,128]{3,2,1,0:T(8,128)(2,1)S(1)} %slice.75), channel_id=1, source_target_pairs={{0,96},{8,104},{16,112},{24,120},{32,0},{40,8},{48,16},{56,24},{64... | collective-permute-start | bytes 786440 | tf_op jit(solution)/shard_map/ppermute | solution.py:217
  109.6 8.6 %copy-start.7 = (bf16[8,1,128,128]{3,2,1,0:T(8,128)(2,1)}, bf16[8,1,128,128]{3,2,1,0:T(8,128)(2,1)S(1)}, u32[]{:S(2)}) copy-start(bf16[8,1,128,128]{3,2,1,0:T(8,128)(2,1)S(1)} %collective-permute-done.8.refs_4_) | copy-start | bytes 786436
  109.6 8.3 %collective-permute-start.12 = (bf16[8,1,128,128]{3,2,1,0:T(8,128)(2,1)S(1)}, bf16[8,1,128,128]{3,2,1,0:T(8,128)(2,1)S(1)}, u32[]{:S(2)}, u32[]{:S(2)}) collective-permute-start(bf16[8,1,128,128]{3,2,1,0:T(8,128)(2,1)S(1)} %collective-permute-done.8.refs_4_), channel_id=1, source_target_pairs={{0,8},{8,0},{16,24},{24,16},{32,40},{40,32},{48,56},{56,48},{64,72... | collective-permute-start | bytes 786440 | tf_op jit(solution)/shard_map/ppermute | solution.py:211
  116.1 2.2 %copy-start.8 = (bf16[8,1,128,128]{3,2,1,0:T(8,128)(2,1)}, bf16[8,1,128,128]{3,2,1,0:T(8,128)(2,1)S(1)}, u32[]{:S(2)}) copy-start(bf16[8,1,128,128]{3,2,1,0:T(8,128)(2,1)S(1)} %collective-permute-done.9.refs_5_) | copy-start | bytes 786436
  116.1 2.2 %collective-permute-start.13 = (bf16[8,1,128,128]{3,2,1,0:T(8,128)(2,1)S(1)}, bf16[8,1,128,128]{3,2,1,0:T(8,128)(2,1)S(1)}, u32[]{:S(2)}, u32[]{:S(2)}) collective-permute-start(bf16[8,1,128,128]{3,2,1,0:T(8,128)(2,1)S(1)} %collective-permute-done.9.refs_5_), channel_id=1, source_target_pairs={{0,8},{8,0},{16,24},{24,16},{32,40},{40,32},{48,56},{56,48},{64,72... | collective-permute-start | bytes 786440 | tf_op jit(solution)/shard_map/ppermute | solution.py:211
  117.1 0.8 copy-start.4
  117.1 1.2 copy-start.5
  117.9 0.8 copy-start.6
  117.9 0.9 copy-start.9
  118.2 0.7 copy-start.10
where the time goes:
time: 135 us; the launch traced here: 134 us
  starting transfers between devices  41.5 us (31%)
  Pallas kernels  33.8 us (25%)
  waiting for transfers between devices  23.6 us (17%)
  other arithmetic  18.5 us (14%)
  blocking collectives  14.9 us (11%)
  local copies, waits for them, and re-layouts  1.61 us (1%)
    pallas_call x1, Pallas kernels, local(): pl.pallas_call(synthesis_kernel, in_specs=[smem, vmem, pl.BlockSpec(memor...  18.5 us
    ppermute x6, starting transfers between devices, to_core(): return lax.ppermute(x, 'member', [(e, e ^ 1) for e in ring])  15.7 us
    pallas_call x1, Pallas kernels, local(): pl.pallas_call(functools.partial(perturb_kernel, groups), grid=(channels...  15.2 us
    all_to_all x1, blocking collectives, local(): lax.all_to_all(mean, 'space', split_axis=0, concat_axis=0, tiled=True)  14.9 us
    ppermute x8, starting transfers between devices, along_z(): lax.ppermute(x, 'member', [(e, (e + 4 * steps) % members) for e in ring])  14.2 us
    ppermute x8, waiting for transfers between devices, along_z(): lax.ppermute(x, 'member', [(e, (e + 4 * steps) % members) for e in ring])  12.4 us
    ppermute x1, waiting for transfers between devices, to_chip(): return lax.ppermute(x, 'member', [(e, e ^ 2) for e in ring])  10.8 us
    another operation x1, other arithmetic  10.7 us
  transfers between devices with their start and end apart: 17, of which 6 were waited for; matrix products, arithmetic and copies ran while one was open for 13% of the time, Pallas kernels for 0%

commit v1 on v0

--- a/solution.py
+++ b/solution.py
@@ -69,12 +69,14 @@
         for h in range(2):
             uni[h, pl.ds(m, pairs, stride=UNI_PITCH), :] = fourier[:, 128 * h : 128 * h + 128]
 
-    def sum_two(turn, carry):
-        sum_degrees(2 * turn)
-        sum_degrees(2 * turn + 1)
+    def sum_four(turn, carry):
+        for u in range(4):
+            sum_degrees(4 * turn + u)
         return carry
 
-    lax.fori_loop(0, order_local // 2, sum_two, 0)
+    lax.fori_loop(0, order_local // 4, sum_four, 0)
+    for m in range(order_local - order_local % 4, order_local):
+        sum_degrees(m)
     blank = jnp.zeros((pairs, 128), F32)
     for h in range(2):
         for m in range(order_local, SLOTS):

time: 135 us -> 133 us (0.985)
  no operation moved by 1% of the time
where the time goes in v1:
time: 133 us
  starting transfers between devices  41.5 us (31%)
  Pallas kernels  32.6 us (25%)
  waiting for transfers between devices  23.6 us (18%)
  other arithmetic  18.5 us (14%)
  blocking collectives  14.9 us (11%)
  local copies, waits for them, and re-layouts  1.61 us (1%)
    pallas_call x1, Pallas kernels, local(): pl.pallas_call(synthesis_kernel, in_specs=[smem, vmem, pl.BlockSpec(memor...  17.3 us
    ppermute x6, starting transfers between devices, to_core(): return lax.ppermute(x, 'member', [(e, e ^ 1) for e in ring])  15.7 us
    pallas_call x1, Pallas kernels, local(): pl.pallas_call(functools.partial(perturb_kernel, groups), grid=(channels...  15.2 us
    all_to_all x1, blocking collectives, local(): lax.all_to_all(mean, 'space', split_axis=0, concat_axis=0, tiled=True)  14.9 us
    ppermute x8, starting transfers between devices, along_z(): lax.ppermute(x, 'member', [(e, (e + 4 * steps) % members) for e in ring])  14.2 us
    ppermute x8, waiting for transfers between devices, along_z(): lax.ppermute(x, 'member', [(e, (e + 4 * steps) % members) for e in ring])  12.4 us
    ppermute x1, waiting for transfers between devices, to_chip(): return lax.ppermute(x, 'member', [(e, e ^ 2) for e in ring])  10.8 us
    another operation x1, other arithmetic  10.7 us
  transfers between devices with their start and end apart: 17, of which 6 were waited for; matrix products, arithmetic and copies ran while one was open for 13% of the time, Pallas kernels for 0%

profile of v1, /device:TPU:1, one launch (start us, length us, event | category | flops | bytes accessed | tf_op | source)
XLA Modules:
  0.0 132.9 jit_solution(2488507696823575828)
XLA Ops:
  0.1 0.2 select_reduce_fusion
  0.3 0.7 pad_add_fusion.first_ref.me_ref
  1.0 0.1 add_exponential_fusion
  1.1 0.6 pad_maximum_fusion.3.table_ref
  1.7 17.3 %synthesis.1 = (bf16[8,10,128,128]{3,2,1,0:T(8,128)(2,1)}, bf16[8,6,128,128]{3,2,1,0:T(8,128)(2,1)}, bf16[8,8,128,128]{3,2,1,0:T(8,128)(2,1)}) custom-call(s32[2]{0:T(128)} %pad_add_fusion.first_ref.me_ref, f32[56,256]{1,0:T(8,128)} %pad_maximum_fusion.3.table_ref, s32[84,46,2,361]{3,2,1,0:T(2,128)} %bitcast.8), custom_call_target="tpu_custom_call" | custom-call | tf_op jit(solution)/shard_map/synthesis/pallas_call | solution.py:222
  19.0 1.6 %collective-permute-start = (bf16[8,8,128,128]{3,2,1,0:T(8,128)(2,1)}, bf16[8,8,128,128]{3,2,1,0:T(8,128)(2,1)}, u32[]{:S(2)}, u32[]{:S(2)}) collective-permute-start(bf16[8,8,128,128]{3,2,1,0:T(8,128)(2,1)} %get-tuple-element.15), channel_id=1, source_target_pairs={{0,8},{8,0},{16,24},{24,16},{32,40},{40,32},{48,56},{56,48},{64,72... | collective-permute-start | bytes 6291464 | tf_op jit(solution)/shard_map/ppermute | solution.py:213
  20.6 6.8 %all-to-all-start = ((bf16[8,10,128,128]{3,2,1,0:T(8,128)(2,1)}), bf16[8,10,128,128]{3,2,1,0:T(8,128)(2,1)S(1)}, u32[]{:S(2)}, u32[]{:S(2)}) async-start(bf16[8,10,128,128]{3,2,1,0:T(8,128)(2,1)} %get-tuple-element.14), calls=%async_computation | async-start | bytes 5242880 | tf_op jit(solution)/shard_map/all_to_all | solution.py:238
  27.4 0.1 iota_add_fusion
  27.5 2.9 %add_convert_fusion.3 = (bf16[8,2,128,128]{3,2,1,0:T(8,128)(2,1)S(1)}, bf16[8,2,128,128]{3,2,1,0:T(8,128)(2,1)S(1)}, bf16[8,2,128,128]{3,2,1,0:T(8,128)(2,1)S(1)}, bf16[8,2,128,128]{3,2,1,0:T(8,128)(2,1)S(1)}) fusion(bf16[8,8,128,128]{3,2,1,0:T(8,128)(2,1)} %collective-permute-done, bf16[8,10,128,128]{3,2,1,0:T(8,128)(2,1)} %get-tuple-element.14), kind=kLoop, calls=%fused_computation.14 | loop fusion | flops 4194304 | bytes 6291456 | tf_op jit(solution)/shard_map/convert_element_type | solution.py:240
  30.4 3.8 %collective-permute-start.3 = (bf16[8,1,128,128]{3,2,1,0:T(8,128)(2,1)S(1)}, bf16[8,1,128,128]{3,2,1,0:T(8,128)(2,1)S(1)}, u32[]{:S(2)}, u32[]{:S(2)}) collective-permute-start(bf16[8,1,128,128]{3,2,1,0:T(8,128)(2,1)S(1)} %get-tuple-element.28), channel_id=1, source_target_pairs={{0,96},{8,104},{16,112},{24,120},{32,0},{40,8},{48,16},{56,24},{64... | collective-permute-start | bytes 786440 | tf_op jit(solution)/shard_map/ppermute | solution.py:219
  34.2 0.1 select_select_fusion
  34.3 0.1 collective-permute-start.1
  34.4 5.1 %collective-permute-done.3 = bf16[8,1,128,128]{3,2,1,0:T(8,128)(2,1)S(1)} collective-permute-done((bf16[8,1,128,128]{3,2,1,0:T(8,128)(2,1)S(1)}, bf16[8,1,128,128]{3,2,1,0:T(8,128)(2,1)S(1)}, u32[]{:S(2)}, u32[]{:S(2)}) %collective-permute-start.3) | collective-permute-done | bytes 262176 | tf_op jit(solution)/shard_map/ppermute | solution.py:219
  39.6 0.1 add_convert_fusion.5
  39.6 0.1 pad_maximum_fusion.2
  39.7 3.5 %collective-permute-start.4 = (bf16[8,2,128,128]{3,2,1,0:T(8,128)(2,1)S(1)}, bf16[8,2,128,128]{3,2,1,0:T(8,128)(2,1)S(1)}, u32[]{:S(2)}, u32[]{:S(2)}) collective-permute-start(bf16[8,2,128,128]{3,2,1,0:T(8,128)(2,1)S(1)} %pad_maximum_fusion.2), channel_id=1, source_target_pairs={{0,96},{8,104},{16,112},{24,120},{32,0},{40,8},{48,16},{56,24},{64... | collective-permute-start | bytes 1572872 | tf_op jit(solution)/shard_map/ppermute | solution.py:219
  43.2 0.0 collective-permute-done.1
  43.2 0.1 add_convert_fusion.6
  43.3 0.1 pad_maximum_fusion.1
  43.3 0.1 collective-permute-start.2
  43.4 10.7 %multiply_convert_fusion.1 = (bf16[8,1,48,1440]{3,2,1,0:T(8,128)(2,1)S(1)}, bf16[8,1,48,1440]{3,2,1,0:T(8,128)(2,1)S(1)}) fusion(s32[8,48]{1,0:T(8,128)S(1)} %iota_add_fusion, f32[8,48]{1,0:T(8,128)S(1)} %select_select_fusion), kind=kLoop, calls=%fused_computation.5 | loop fusion | flops 7188480 | bytes 2214912 | tf_op jit(solution)/shard_map/convert
  54.1 1.7 %pad_maximum_fusion = bf16[8,2,48,1440]{3,2,1,0:T(8,128)(2,1)} fusion(bf16[8,1,48,1440]{3,2,1,0:T(8,128)(2,1)S(1)} %get-tuple-element.30, bf16[8,1,48,1440]{3,2,1,0:T(8,128)(2,1)S(1)} %get-tuple-element.29), kind=kLoop, calls=%fused_computation.3 | loop fusion | flops 1105920 | bytes 4423680 | tf_op jit(solution)/shard_map/stack | solution.py:192
  55.8 0.0 collective-permute-done.4
  55.8 0.9 collective-permute-done.2
  56.6 0.2 add_convert_fusion
  56.9 0.4 collective-permute-start.5
  57.3 10.8 %collective-permute-done.5 = bf16[8,2,128,128]{3,2,1,0:T(8,128)(2,1)S(1)} collective-permute-done((bf16[8,2,128,128]{3,2,1,0:T(8,128)(2,1)S(1)}, bf16[8,2,128,128]{3,2,1,0:T(8,128)(2,1)S(1)}, u32[]{:S(2)}, u32[]{:S(2)}) %collective-permute-start.5) | collective-permute-done | bytes 524320 | tf_op jit(solution)/shard_map/ppermute | solution.py:216
  68.1 1.0 multiply_convert_fusion.2
  69.1 14.9 %all_to_all.15.refs_2_ = bf16[8,2,128,128]{3,2,1,0:T(8,128)(2,1)S(1)} all-to-all(bf16[8,2,128,128]{3,2,1,0:T(8,128)(2,1)} %multiply_convert_fusion.2), channel_id=1, replica_groups=mesh['member'=16,'space'=8] {'space'}, dimensions={0} | all-to-all | bytes 1048576 | tf_op jit(solution)/shard_map/all_to_all | solution.py:252
  84.0 4.3 %all-to-all-start.2 = ((bf16[8,6,128,128]{3,2,1,0:T(8,128)(2,1)}), bf16[8,6,128,128]{3,2,1,0:T(8,128)(2,1)}, u32[]{:S(2)}, u32[]{:S(2)}) async-start(bf16[8,6,128,128]{3,2,1,0:T(8,128)(2,1)} %get-tuple-element.21), calls=%async_computation.2 | async-start | bytes 3145728 | tf_op jit(solution)/shard_map/all_to_all | solution.py:254
  88.3 2.2 %collective-permute-start.7 = (bf16[8,2,128,128]{3,2,1,0:T(8,128)(2,1)S(1)}, bf16[8,2,128,128]{3,2,1,0:T(8,128)(2,1)S(1)}, u32[]{:S(2)}, u32[]{:S(2)}) collective-permute-start(bf16[8,2,128,128]{3,2,1,0:T(8,128)(2,1)S(1)} %all_to_all.15.refs_2_), channel_id=1, source_target_pairs={{0,32},{8,40},{16,48},{24,56},{32,64},{40,72},{48,80},{56,88},{64,... | collective-permute-start | bytes 1572872 | tf_op jit(solution)/shard_map/ppermute | solution.py:219
  90.6 1.7 %collective-permute-start.6 = (bf16[8,2,128,128]{3,2,1,0:T(8,128)(2,1)S(1)}, bf16[8,2,128,128]{3,2,1,0:T(8,128)(2,1)S(1)}, u32[]{:S(2)}, u32[]{:S(2)}) collective-permute-start(bf16[8,2,128,128]{3,2,1,0:T(8,128)(2,1)S(1)} %all_to_all.15.refs_2_), channel_id=1, source_target_pairs={{0,96},{8,104},{16,112},{24,120},{32,0},{40,8},{48,16},{56,24},{64... | collective-permute-start | bytes 1572872 | tf_op jit(solution)/shard_map/ppermute | solution.py:219
  92.3 4.1 %collective-permute-start.10 = (bf16[8,2,128,128]{3,2,1,0:T(8,128)(2,1)S(1)}, bf16[8,2,128,128]{3,2,1,0:T(8,128)(2,1)S(1)}, u32[]{:S(2)}, u32[]{:S(2)}) collective-permute-start(bf16[8,2,128,128]{3,2,1,0:T(8,128)(2,1)S(1)} %all_to_all.15.refs_2_), channel_id=1, source_target_pairs={{0,8},{8,0},{16,24},{24,16},{32,40},{40,32},{48,56},{56,48},{64,72... | collective-permute-start | bytes 1572872 | tf_op jit(solution)/shard_map/ppermute | solution.py:213
  96.4 4.4 %collective-permute-done.7.refs_6_ = bf16[8,2,128,128]{3,2,1,0:T(8,128)(2,1)S(1)} collective-permute-done((bf16[8,2,128,128]{3,2,1,0:T(8,128)(2,1)S(1)}, bf16[8,2,128,128]{3,2,1,0:T(8,128)(2,1)S(1)}, u32[]{:S(2)}, u32[]{:S(2)}) %collective-permute-start.7) | collective-permute-done | bytes 524320 | tf_op jit(solution)/shard_map/ppermute | solution.py:219
  100.8 0.8 collective-permute-start.8
  101.6 4.6 %collective-permute-start.14 = (bf16[8,2,128,128]{3,2,1,0:T(8,128)(2,1)S(1)}, bf16[8,2,128,128]{3,2,1,0:T(8,128)(2,1)S(1)}, u32[]{:S(2)}, u32[]{:S(2)}) collective-permute-start(bf16[8,2,128,128]{3,2,1,0:T(8,128)(2,1)S(1)} %collective-permute-done.7.refs_6_), channel_id=1, source_target_pairs={{0,8},{8,0},{16,24},{24,16},{32,40},{40,32},{48,56},{56,48},{64,72... | collective-permute-start | bytes 1572872 | tf_op jit(solution)/shard_map/ppermute | solution.py:213
  106.2 0.0 collective-permute-done.6.refs_3_
  106.2 0.1 collective-permute-start.11
  106.3 2.1 %collective-permute-start.9 = (bf16[8,1,128,128]{3,2,1,0:T(8,128)(2,1)S(1)}, bf16[8,1,128,128]{3,2,1,0:T(8,128)(2,1)S(1)}, u32[]{:S(2)}, u32[]{:S(2)}) collective-permute-start(bf16[8,1,128,128]{3,2,1,0:T(8,128)(2,1)S(1)} %slice.75), channel_id=1, source_target_pairs={{0,96},{8,104},{16,112},{24,120},{32,0},{40,8},{48,16},{56,24},{64... | collective-permute-start | bytes 786440 | tf_op jit(solution)/shard_map/ppermute | solution.py:219
  108.4 4.4 %collective-permute-start.12 = (bf16[8,1,128,128]{3,2,1,0:T(8,128)(2,1)S(1)}, bf16[8,1,128,128]{3,2,1,0:T(8,128)(2,1)S(1)}, u32[]{:S(2)}, u32[]{:S(2)}) collective-permute-start(bf16[8,1,128,128]{3,2,1,0:T(8,128)(2,1)S(1)} %collective-permute-done.8.refs_4_), channel_id=1, source_target_pairs={{0,8},{8,0},{16,24},{24,16},{32,40},{40,32},{48,56},{56,48},{64,72... | collective-permute-start | bytes 786440 | tf_op jit(solution)/shard_map/ppermute | solution.py:213
  112.8 2.0 %collective-permute-done.9.refs_5_ = bf16[8,1,128,128]{3,2,1,0:T(8,128)(2,1)S(1)} collective-permute-done((bf16[8,1,128,128]{3,2,1,0:T(8,128)(2,1)S(1)}, bf16[8,1,128,128]{3,2,1,0:T(8,128)(2,1)S(1)}, u32[]{:S(2)}, u32[]{:S(2)}) %collective-permute-start.9) | collective-permute-done | bytes 262176 | tf_op jit(solution)/shard_map/ppermute | solution.py:219
  114.8 1.0 collective-permute-start.13
  115.9 0.8 copy-done.4
  116.7 0.3 collective-permute-done.13.refs_10_
  117.0 0.4 copy-done.6
  117.5 0.1 copy-done.9
  117.6 0.1 copy-done.10
  117.7 15.2 %perturb.1 = bf16[84,32,1440]{2,1,0:T(8,128)(2,1)} custom-call(f32[84]{0:T(128)} %scale_ref.1, s32[2]{0:T(128)} %pad_add_fusion.first_ref.me_ref, bf16[768,1440]{1,0:T(8,128)(2,1)} %bitcast.9, bf16[84,32,1440]{2,1,0:T(8,128)(2,1)} %bitcast.10, bf16[8,10,128,128]{3,2,1,0:T(8,128)(2,1)} %copy-done, bf16[8,6,128,128]{3,2,1,0:T(8,128)(2,1)} %all-to-all-done.2.refs_1_, ...), custom_call_target="tpu_custom_call" | custom-call | tf_op jit(solution)/shard_map/perturb/pallas_call | solution.py:268
  (40 shorter events, 0.3 us)
Async XLA Ops:
  19.0 8.4 %collective-permute-start = (bf16[8,8,128,128]{3,2,1,0:T(8,128)(2,1)}, bf16[8,8,128,128]{3,2,1,0:T(8,128)(2,1)}, u32[]{:S(2)}, u32[]{:S(2)}) collective-permute-start(bf16[8,8,128,128]{3,2,1,0:T(8,128)(2,1)} %get-tuple-element.15), channel_id=1, source_target_pairs={{0,8},{8,0},{16,24},{24,16},{32,40},{40,32},{48,56},{56,48},{64,72... | collective-permute-start | bytes 6291464 | tf_op jit(solution)/shard_map/ppermute | solution.py:213
  20.6 48.5 %all-to-all-start = ((bf16[8,10,128,128]{3,2,1,0:T(8,128)(2,1)}), bf16[8,10,128,128]{3,2,1,0:T(8,128)(2,1)S(1)}, u32[]{:S(2)}, u32[]{:S(2)}) async-start(bf16[8,10,128,128]{3,2,1,0:T(8,128)(2,1)} %get-tuple-element.14), calls=%async_computation | async-start | bytes 5242880 | tf_op jit(solution)/shard_map/all_to_all | solution.py:238
  30.4 9.1 %collective-permute-start.3 = (bf16[8,1,128,128]{3,2,1,0:T(8,128)(2,1)S(1)}, bf16[8,1,128,128]{3,2,1,0:T(8,128)(2,1)S(1)}, u32[]{:S(2)}, u32[]{:S(2)}) collective-permute-start(bf16[8,1,128,128]{3,2,1,0:T(8,128)(2,1)S(1)} %get-tuple-element.28), channel_id=1, source_target_pairs={{0,96},{8,104},{16,112},{24,120},{32,0},{40,8},{48,16},{56,24},{64... | collective-permute-start | bytes 786440 | tf_op jit(solution)/shard_map/ppermute | solution.py:219
  34.3 8.8 %collective-permute-start.1 = (bf16[8,1,128,128]{3,2,1,0:T(8,128)(2,1)S(1)}, bf16[8,1,128,128]{3,2,1,0:T(8,128)(2,1)S(1)}, u32[]{:S(2)}, u32[]{:S(2)}) collective-permute-start(bf16[8,1,128,128]{3,2,1,0:T(8,128)(2,1)S(1)} %get-tuple-element.27), channel_id=1, source_target_pairs={{0,32},{8,40},{16,48},{24,56},{32,64},{40,72},{48,80},{56,88},{64,... | collective-permute-start | bytes 786440 | tf_op jit(solution)/shard_map/ppermute | solution.py:219
  39.7 16.1 %collective-permute-start.4 = (bf16[8,2,128,128]{3,2,1,0:T(8,128)(2,1)S(1)}, bf16[8,2,128,128]{3,2,1,0:T(8,128)(2,1)S(1)}, u32[]{:S(2)}, u32[]{:S(2)}) collective-permute-start(bf16[8,2,128,128]{3,2,1,0:T(8,128)(2,1)S(1)} %pad_maximum_fusion.2), channel_id=1, source_target_pairs={{0,96},{8,104},{16,112},{24,120},{32,0},{40,8},{48,16},{56,24},{64... | collective-permute-start | bytes 1572872 | tf_op jit(solution)/shard_map/ppermute | solution.py:219
  43.3 13.3 %collective-permute-start.2 = (bf16[8,2,128,128]{3,2,1,0:T(8,128)(2,1)S(1)}, bf16[8,2,128,128]{3,2,1,0:T(8,128)(2,1)S(1)}, u32[]{:S(2)}, u32[]{:S(2)}) collective-permute-start(bf16[8,2,128,128]{3,2,1,0:T(8,128)(2,1)S(1)} %pad_maximum_fusion.1), channel_id=1, source_target_pairs={{0,32},{8,40},{16,48},{24,56},{32,64},{40,72},{48,80},{56,88},{64,... | collective-permute-start | bytes 1572872 | tf_op jit(solution)/shard_map/ppermute | solution.py:219
  56.9 11.3 %collective-permute-start.5 = (bf16[8,2,128,128]{3,2,1,0:T(8,128)(2,1)S(1)}, bf16[8,2,128,128]{3,2,1,0:T(8,128)(2,1)S(1)}, u32[]{:S(2)}, u32[]{:S(2)}) collective-permute-start(bf16[8,2,128,128]{3,2,1,0:T(8,128)(2,1)S(1)} %add_convert_fusion), channel_id=1, source_target_pairs={{0,16},{8,24},{16,0},{24,8},{32,48},{40,56},{48,32},{56,40},{64,80... | collective-permute-start | bytes 1572872 | tf_op jit(solution)/shard_map/ppermute | solution.py:216
  69.1 31.7 %copy-start = (bf16[8,10,128,128]{3,2,1,0:T(8,128)(2,1)}, bf16[8,10,128,128]{3,2,1,0:T(8,128)(2,1)S(1)}, u32[]{:S(2)}) copy-start(bf16[8,10,128,128]{3,2,1,0:T(8,128)(2,1)S(1)} %all-to-all-done.refs_0_) | copy-start | bytes 7864324
  84.0 33.0 %copy-start.1 = (bf16[8,2,128,128]{3,2,1,0:T(8,128)(2,1)}, bf16[8,2,128,128]{3,2,1,0:T(8,128)(2,1)S(1)}, u32[]{:S(2)}) copy-start(bf16[8,2,128,128]{3,2,1,0:T(8,128)(2,1)S(1)} %all_to_all.15.refs_2_) | copy-start | bytes 1572868
  84.0 33.0 %all-to-all-start.2 = ((bf16[8,6,128,128]{3,2,1,0:T(8,128)(2,1)}), bf16[8,6,128,128]{3,2,1,0:T(8,128)(2,1)}, u32[]{:S(2)}, u32[]{:S(2)}) async-start(bf16[8,6,128,128]{3,2,1,0:T(8,128)(2,1)} %get-tuple-element.21), calls=%async_computation.2 | async-start | bytes 3145728 | tf_op jit(solution)/shard_map/all_to_all | solution.py:254
  88.3 12.4 %collective-permute-start.7 = (bf16[8,2,128,128]{3,2,1,0:T(8,128)(2,1)S(1)}, bf16[8,2,128,128]{3,2,1,0:T(8,128)(2,1)S(1)}, u32[]{:S(2)}, u32[]{:S(2)}) collective-permute-start(bf16[8,2,128,128]{3,2,1,0:T(8,128)(2,1)S(1)} %all_to_all.15.refs_2_), channel_id=1, source_target_pairs={{0,32},{8,40},{16,48},{24,56},{32,64},{40,72},{48,80},{56,88},{64,... | collective-permute-start | bytes 1572872 | tf_op jit(solution)/shard_map/ppermute | solution.py:219
  90.6 15.6 %collective-permute-start.6 = (bf16[8,2,128,128]{3,2,1,0:T(8,128)(2,1)S(1)}, bf16[8,2,128,128]{3,2,1,0:T(8,128)(2,1)S(1)}, u32[]{:S(2)}, u32[]{:S(2)}) collective-permute-start(bf16[8,2,128,128]{3,2,1,0:T(8,128)(2,1)S(1)} %all_to_all.15.refs_2_), channel_id=1, source_target_pairs={{0,96},{8,104},{16,112},{24,120},{32,0},{40,8},{48,16},{56,24},{64... | collective-permute-start | bytes 1572872 | tf_op jit(solution)/shard_map/ppermute | solution.py:219
  92.3 23.5 %collective-permute-start.10 = (bf16[8,2,128,128]{3,2,1,0:T(8,128)(2,1)S(1)}, bf16[8,2,128,128]{3,2,1,0:T(8,128)(2,1)S(1)}, u32[]{:S(2)}, u32[]{:S(2)}) collective-permute-start(bf16[8,2,128,128]{3,2,1,0:T(8,128)(2,1)S(1)} %all_to_all.15.refs_2_), channel_id=1, source_target_pairs={{0,8},{8,0},{16,24},{24,16},{32,40},{40,32},{48,56},{56,48},{64,72... | collective-permute-start | bytes 1572872 | tf_op jit(solution)/shard_map/ppermute | solution.py:213
  100.8 15.0 %copy-start.2 = (bf16[8,2,128,128]{3,2,1,0:T(8,128)(2,1)}, bf16[8,2,128,128]{3,2,1,0:T(8,128)(2,1)S(1)}, u32[]{:S(2)}) copy-start(bf16[8,2,128,128]{3,2,1,0:T(8,128)(2,1)S(1)} %collective-permute-done.7.refs_6_) | copy-start | bytes 1572868
  100.8 7.5 %collective-permute-start.8 = (bf16[8,1,128,128]{3,2,1,0:T(8,128)(2,1)S(1)}, bf16[8,1,128,128]{3,2,1,0:T(8,128)(2,1)S(1)}, u32[]{:S(2)}, u32[]{:S(2)}) collective-permute-start(bf16[8,1,128,128]{3,2,1,0:T(8,128)(2,1)S(1)} %slice.74), channel_id=1, source_target_pairs={{0,32},{8,40},{16,48},{24,56},{32,64},{40,72},{48,80},{56,88},{64,... | collective-permute-start | bytes 786440 | tf_op jit(solution)/shard_map/ppermute | solution.py:219
  101.6 14.2 %collective-permute-start.14 = (bf16[8,2,128,128]{3,2,1,0:T(8,128)(2,1)S(1)}, bf16[8,2,128,128]{3,2,1,0:T(8,128)(2,1)S(1)}, u32[]{:S(2)}, u32[]{:S(2)}) collective-permute-start(bf16[8,2,128,128]{3,2,1,0:T(8,128)(2,1)S(1)} %collective-permute-done.7.refs_6_), channel_id=1, source_target_pairs={{0,8},{8,0},{16,24},{24,16},{32,40},{40,32},{48,56},{56,48},{64,72... | collective-permute-start | bytes 1572872 | tf_op jit(solution)/shard_map/ppermute | solution.py:213
  106.2 9.7 %copy-start.3 = (bf16[8,2,128,128]{3,2,1,0:T(8,128)(2,1)}, bf16[8,2,128,128]{3,2,1,0:T(8,128)(2,1)S(1)}, u32[]{:S(2)}) copy-start(bf16[8,2,128,128]{3,2,1,0:T(8,128)(2,1)S(1)} %collective-permute-done.6.refs_3_) | copy-start | bytes 1572868
  106.2 9.7 %collective-permute-start.11 = (bf16[8,2,128,128]{3,2,1,0:T(8,128)(2,1)S(1)}, bf16[8,2,128,128]{3,2,1,0:T(8,128)(2,1)S(1)}, u32[]{:S(2)}, u32[]{:S(2)}) collective-permute-start(bf16[8,2,128,128]{3,2,1,0:T(8,128)(2,1)S(1)} %collective-permute-done.6.refs_3_), channel_id=1, source_target_pairs={{0,8},{8,0},{16,24},{24,16},{32,40},{40,32},{48,56},{56,48},{64,72... | collective-permute-start | bytes 1572872 | tf_op jit(solution)/shard_map/ppermute | solution.py:213
  106.3 8.5 %collective-permute-start.9 = (bf16[8,1,128,128]{3,2,1,0:T(8,128)(2,1)S(1)}, bf16[8,1,128,128]{3,2,1,0:T(8,128)(2,1)S(1)}, u32[]{:S(2)}, u32[]{:S(2)}) collective-permute-start(bf16[8,1,128,128]{3,2,1,0:T(8,128)(2,1)S(1)} %slice.75), channel_id=1, source_target_pairs={{0,96},{8,104},{16,112},{24,120},{32,0},{40,8},{48,16},{56,24},{64... | collective-permute-start | bytes 786440 | tf_op jit(solution)/shard_map/ppermute | solution.py:219
  108.4 8.6 %copy-start.7 = (bf16[8,1,128,128]{3,2,1,0:T(8,128)(2,1)}, bf16[8,1,128,128]{3,2,1,0:T(8,128)(2,1)S(1)}, u32[]{:S(2)}) copy-start(bf16[8,1,128,128]{3,2,1,0:T(8,128)(2,1)S(1)} %collective-permute-done.8.refs_4_) | copy-start | bytes 786436
  108.4 8.3 %collective-permute-start.12 = (bf16[8,1,128,128]{3,2,1,0:T(8,128)(2,1)S(1)}, bf16[8,1,128,128]{3,2,1,0:T(8,128)(2,1)S(1)}, u32[]{:S(2)}, u32[]{:S(2)}) collective-permute-start(bf16[8,1,128,128]{3,2,1,0:T(8,128)(2,1)S(1)} %collective-permute-done.8.refs_4_), channel_id=1, source_target_pairs={{0,8},{8,0},{16,24},{24,16},{32,40},{40,32},{48,56},{56,48},{64,72... | collective-permute-start | bytes 786440 | tf_op jit(solution)/shard_map/ppermute | solution.py:213
  114.8 2.2 %copy-start.8 = (bf16[8,1,128,128]{3,2,1,0:T(8,128)(2,1)}, bf16[8,1,128,128]{3,2,1,0:T(8,128)(2,1)S(1)}, u32[]{:S(2)}) copy-start(bf16[8,1,128,128]{3,2,1,0:T(8,128)(2,1)S(1)} %collective-permute-done.9.refs_5_) | copy-start | bytes 786436
  114.8 2.2 %collective-permute-start.13 = (bf16[8,1,128,128]{3,2,1,0:T(8,128)(2,1)S(1)}, bf16[8,1,128,128]{3,2,1,0:T(8,128)(2,1)S(1)}, u32[]{:S(2)}, u32[]{:S(2)}) collective-permute-start(bf16[8,1,128,128]{3,2,1,0:T(8,128)(2,1)S(1)} %collective-permute-done.9.refs_5_), channel_id=1, source_target_pairs={{0,8},{8,0},{16,24},{24,16},{32,40},{40,32},{48,56},{56,48},{64,72... | collective-permute-start | bytes 786440 | tf_op jit(solution)/shard_map/ppermute | solution.py:213
  115.8 0.8 copy-start.4
  115.8 1.2 copy-start.5
  116.7 0.8 copy-start.6
  116.7 0.9 copy-start.9
  117.0 0.7 copy-start.10
